TPU v7x, 32 devices: a whole 2x2x4 slice. The times are simulated.
32 devices in a mesh: rows: 8 (over z, y), cols: 4 (over x, core).
Axes of the slice: x: 2, y: 2, z: 4, core: 2. Of those that a mesh axis runs over, the one named last changes fastest.
Arguments:
- gradients: float32 [32, 128, 4096], P(None, 'rows', 'cols'), may hold values from -6 to 6
- momentum: float32 [32, 128, 4096], P(None, 'rows', 'cols'), may hold values from -6 to 6
- weights: float32 [32, 128, 4096], P(None, 'rows', 'cols'), may hold values from -0.1875 to 0.1875
Outputs:
- new_weights: float32 [32, 128, 4096], P(None, 'rows', 'cols')
- new_momentum: float32 [32, 128, 4096], P(None, 'rows', 'cols')
All inputs are finite; a program needn't handle non-finite values.
Results may differ from a plain program's by a relative error of at most 0.0003.
Values sent between devices are 32-bit elements.
A program may use at most 64 MiB of HBM per device.

v0:
```python
import jax
import jax.numpy as jnp
from jax import lax
from jax.sharding import PartitionSpec as P

ITERS = 4
hold_rate = 0.8
learn_rate = 0.8
decay_rate = 0.1


def mul(a, b):
    return jnp.einsum("mij,mjk->mik", a, b, precision=lax.Precision.HIGHEST)


def local(gradients, momentum, weights):
    new_momentum = hold_rate * momentum + gradients
    whole = lax.all_to_all(new_momentum, "rows", split_axis=0, concat_axis=1, tiled=True)
    gram = jnp.einsum("mik,mjk->mij", whole, whole, precision=lax.Precision.HIGHEST)
    gram = lax.psum(gram, "cols")
    eye = jnp.eye(gram.shape[-1], dtype=jnp.float32)
    total = jnp.sum(gram * eye, axis=(1, 2), keepdims=True)
    scale = lax.rsqrt(total + 1e-06)
    gram = gram * scale * scale
    chain = scale * eye
    for step in range(ITERS):
        factor = 3.4445 * eye - 4.775 * gram + 2.0315 * mul(gram, gram)
        chain = mul(factor, chain)
        if step < ITERS - 1:
            gram = mul(factor, mul(gram, factor))
    iterate = mul(chain, whole)
    back = lax.all_to_all(iterate, "rows", split_axis=1, concat_axis=0, tiled=True)
    new_weights = (1.0 - learn_rate * decay_rate) * weights - learn_rate * back
    return (new_weights, new_momentum)


def solution(mesh):
    placed = (P(None, "rows", "cols"), P(None, "rows", "cols"), P(None, "rows", "cols"))
    return jax.shard_map(
        local,
        mesh=mesh,
        in_specs=placed,
        out_specs=(P(None, "rows", "cols"), P(None, "rows", "cols")),
        check_vma=False,
    )
```

profile of v0, /device:TPU:0, one launch (start us, length us, event | category | flops | bytes accessed | tf_op | source)
XLA Modules:
  0.0 175.1 jit_solution(10635801916381420988)
XLA Ops:
  7.2 0.0 all-reduce.2.cloned.1.call-start
  7.2 2.7 %multiply_add_fusion = f32[32,16,1024]{2,1,0:T(8,128)S(1)} fusion(f32[32,16,1024]{2,1,0:T(8,128)} %param.3, f32[32,16,1024]{2,1,0:T(8,128)} %param.4), kind=kLoop, calls=%fused_computation.1 | loop fusion | flops 1048576 | bytes 6291456 | tf_op jit(solution)/shard_map/add | solution.py:17
  9.9 0.0 copy-start
  9.9 55.3 %all_to_all.27 = f32[32,16,1024]{2,1,0:T(8,128)S(1)} all-to-all(f32[32,16,1024]{2,1,0:T(8,128)S(1)} %multiply_add_fusion), channel_id=1, replica_groups=mesh['rows'=8,'cols'=4] {'rows'}, dimensions={0} | all-to-all | bytes 4194304 | tf_op jit(solution)/shard_map/all_to_all | solution.py:18
  65.2 0.0 copy-done
  65.2 0.1 copy.7
  65.4 2.8 %fusion.13 = f32[4,128,128]{2,1,0:T(8,128)} fusion(f32[4,128,1024]{2,1,0:T(8,128)S(1)} %bitcast.37), kind=kOutput, calls=%fused_computation.24 | convolution fusion | flops 805306368 | bytes 2359296 | tf_op jit(solution)/shard_map/mik,mjk->mij/dot_general | solution.py:19
  68.1 0.0 all-reduce.2.cloned.1.call-update
  68.2 31.4 %all-reduce.2.cloned.1.call-done = f32[4,128,128]{2,1,0:T(8,128)} async-done(((f32[4,128,128]{2,1,0:T(8,128)}), f32[4,128,128]{2,1,0:T(8,128)}) %all-reduce.2.cloned.1.call-update) | async-done | bytes 262160 | tf_op jit(solution)/shard_map/psum | solution.py:20
  99.6 1.1 multiply_reduce_fusion
  100.7 1.6 fusion.3
  102.3 0.4 fusion.4
  102.7 1.4 fusion.6
  104.1 0.4 fusion.14
  104.5 0.4 fusion.2
  104.9 0.4 fusion.15
  105.3 0.4 fusion.19
  105.7 0.4 fusion.16
  106.1 0.4 fusion.1
  106.5 0.4 fusion.17
  106.9 0.4 fusion.20
  107.3 0.4 fusion.18
  107.7 0.4 fusion
  108.1 0.4 fusion.21
  108.5 1.9 %fusion.22 = f32[4,128,1024]{2,1,0:T(8,128)S(1)} fusion(f32[4,128,128]{2,1,0:T(8,128)S(1)} %fusion.21, f32[4,128,1024]{2,1,0:T(8,128)S(1)} %bitcast.38), kind=kOutput, calls=%fused_computation.33 | convolution fusion | flops 805306368 | bytes 4456448 | tf_op jit(solution)/shard_map/mij,mjk->mik/dot_general | solution.py:13
  110.4 1.4 copy.8
  111.8 52.5 %all_to_all.28 = f32[4,128,1024]{2,0,1:T(4,128)S(1)} all-to-all(f32[4,128,1024]{2,0,1:T(4,128)S(1)} %copy.8), channel_id=1, replica_groups=mesh['rows'=8,'cols'=4] {'rows'}, dimensions={1} | all-to-all | bytes 4194304 | tf_op jit(solution)/shard_map/all_to_all | solution.py:32
  164.3 0.6 broadcast_multiply_fusion
  164.9 0.0 copy-start.1
  164.9 1.2 copy.9
  166.1 0.4 copy-done.1
  166.5 1.8 %bitcast_subtract_fusion = f32[32,16,1024]{2,1,0:T(8,128)} fusion(f32[8,4,16,1024]{3,2,1,0:T(8,128)S(1)} %copy.9, f32[32,16,1024]{2,1,0:T(8,128)S(1)} %copy-done.1), kind=kLoop, calls=%fused_computation | loop fusion | flops 1048576 | bytes 6291456 | tf_op jit(solution)/shard_map/sub | solution.py:33
  (3 shorter events, 0.0 us)
Async XLA Ops:
  7.2 92.4 %all-reduce.2.cloned.1.call-start = ((), (), s32[]{:S(2)}) async-start(), calls=%async_computation.2 | async-start | bytes 524288 | tf_op jit(solution)/shard_map/psum | solution.py:20
  9.9 55.4 %copy-start = (f32[32,16,1024]{2,1,0:T(8,128)}, f32[32,16,1024]{2,1,0:T(8,128)S(1)}, u32[]{:S(2)}) copy-start(f32[32,16,1024]{2,1,0:T(8,128)S(1)} %multiply_add_fusion) | copy-start | bytes 6291460
  164.9 1.6 copy-start.1
Sparse Core Ops, SparseCore 0:
  68.3 31.2 all-reduce.1
where the time goes:
time: 175 us
  blocking collectives  108 us (62%)
  waiting for transfers between devices  31.4 us (18%)
  between operations  14.2 us (8%)
  matrix products  12.4 us (7%)
  other arithmetic  6.1 us (3%)
  local copies, waits for them, and re-layouts  3.07 us (2%)
    all_to_all x1, blocking collectives, local(): lax.all_to_all(new_momentum, 'rows', split_axis=0, concat_axis=1, tiled=T...  55.3 us
    all_to_all x1, blocking collectives, local(): lax.all_to_all(iterate, 'rows', split_axis=1, concat_axis=0, tiled=True)  52.5 us
    psum x1, waiting for transfers between devices, local(): gram = lax.psum(gram, 'cols')  31.4 us
    dot_general x15, matrix products, mul(): return jnp.einsum('mij,mjk->mik', a, b, precision=lax.Precision.HIGHEST)  9.64 us
  transfers between devices with their start and end apart: 1, of which 1 were waited for; matrix products, arithmetic and copies ran while one was open for 0% of the time, Pallas kernels for 0%

commit v1 on v0

--- a/solution.py
+++ b/solution.py
@@ -15,7 +15,9 @@
 
 def local(gradients, momentum, weights):
     new_momentum = hold_rate * momentum + gradients
-    whole = lax.all_to_all(new_momentum, "rows", split_axis=0, concat_axis=1, tiled=True)
+    pieces = jnp.split(new_momentum, lax.axis_size("rows"), axis=0)
+    received = lax.all_to_all(jnp.stack(pieces), "rows", 0, 0)
+    whole = jnp.concatenate(received, axis=1)
     gram = jnp.einsum("mik,mjk->mij", whole, whole, precision=lax.Precision.HIGHEST)
     gram = lax.psum(gram, "cols")
     eye = jnp.eye(gram.shape[-1], dtype=jnp.float32)

time: 175 us -> 177 us (1.011)
  no operation moved by 1% of the time
where the time goes in v1:
time: 177 us
  blocking collectives  108 us (61%)
  waiting for transfers between devices  31.4 us (18%)
  between operations  14.3 us (8%)
  matrix products  12.4 us (7%)
  other arithmetic  6.28 us (4%)
  local copies, waits for them, and re-layouts  4.32 us (2%)
    all_to_all x1, blocking collectives, local(): received = lax.all_to_all(jnp.stack(pieces), 'rows', 0, 0)  55.3 us
    all_to_all x1, blocking collectives, local(): lax.all_to_all(iterate, 'rows', split_axis=1, concat_axis=0, tiled=True)  52.5 us
    psum x1, waiting for transfers between devices, local(): gram = lax.psum(gram, 'cols')  31.4 us
    dot_general x15, matrix products, mul(): return jnp.einsum('mij,mjk->mik', a, b, precision=lax.Precision.HIGHEST)  9.65 us
  transfers between devices with their start and end apart: 1, of which 1 were waited for; matrix products, arithmetic and copies ran while one was open for 0% of the time, Pallas kernels for 0%

profile of v1, /device:TPU:0, one launch (start us, length us, event | category | flops | bytes accessed | tf_op | source)
XLA Modules:
  0.0 176.5 jit_solution(13294960395621938709)
XLA Ops:
  7.2 0.0 all-reduce.2.cloned.1.call-start
  7.2 2.8 %multiply_add_fusion = f32[32,16,1024]{2,1,0:T(8,128)S(1)} fusion(f32[32,16,1024]{2,1,0:T(8,128)} %param.3, f32[32,16,1024]{2,1,0:T(8,128)} %param.4), kind=kLoop, calls=%fused_computation.1 | loop fusion | flops 1048576 | bytes 6291456 | tf_op jit(solution)/shard_map/add | solution.py:17
  10.0 0.0 copy-start
  10.3 1.1 copy-done
  11.4 55.3 %all_to_all.14 = f32[8,4,16,1024]{3,2,1,0:T(8,128)S(1)} all-to-all(f32[8,4,16,1024]{3,2,1,0:T(8,128)S(1)} %fusion.4), channel_id=1, replica_groups=mesh['rows'=8,'cols'=4] {'rows'}, dimensions={0} | all-to-all | bytes 4194304 | tf_op jit(solution)/shard_map/all_to_all | solution.py:19
  66.7 0.1 copy.7
  66.8 2.8 %fusion.21 = f32[4,128,128]{2,1,0:T(8,128)} fusion(f32[4,128,1024]{2,1,0:T(8,128)S(1)} %bitcast.67), kind=kOutput, calls=%fused_computation.40 | convolution fusion | flops 805306368 | bytes 2359296 | tf_op jit(solution)/shard_map/mik,mjk->mij/dot_general | solution.py:21
  69.6 0.0 all-reduce.2.cloned.1.call-update
  69.7 31.4 %all-reduce.2.cloned.1.call-done = f32[4,128,128]{2,1,0:T(8,128)} async-done(((f32[4,128,128]{2,1,0:T(8,128)}), f32[4,128,128]{2,1,0:T(8,128)}) %all-reduce.2.cloned.1.call-update) | async-done | bytes 262160 | tf_op jit(solution)/shard_map/psum | solution.py:22
  101.1 1.1 multiply_reduce_fusion
  102.1 1.6 fusion.3
  103.8 0.4 fusion.12
  104.2 1.4 fusion.14
  105.6 0.4 fusion.22
  106.0 0.4 fusion.2
  106.4 0.4 fusion.23
  106.8 0.4 fusion.27
  107.2 0.4 fusion.24
  107.6 0.4 fusion.1
  108.0 0.4 fusion.25
  108.4 0.4 fusion.28
  108.8 0.4 fusion.26
  109.2 0.4 fusion
  109.6 0.4 fusion.29
  110.0 1.9 %fusion.30 = f32[4,128,1024]{2,1,0:T(8,128)S(1)} fusion(f32[4,128,128]{2,1,0:T(8,128)S(1)} %fusion.29, f32[4,128,1024]{2,1,0:T(8,128)S(1)} %bitcast.68), kind=kOutput, calls=%fused_computation.49 | convolution fusion | flops 805306368 | bytes 4456448 | tf_op jit(solution)/shard_map/mij,mjk->mik/dot_general | solution.py:13
  111.9 1.4 copy.8
  113.3 52.5 %all_to_all.15 = f32[4,128,1024]{2,0,1:T(4,128)S(1)} all-to-all(f32[4,128,1024]{2,0,1:T(4,128)S(1)} %copy.8), channel_id=1, replica_groups=mesh['rows'=8,'cols'=4] {'rows'}, dimensions={1} | all-to-all | bytes 4194304 | tf_op jit(solution)/shard_map/all_to_all | solution.py:34
  165.7 0.6 broadcast_multiply_fusion
  166.3 0.0 copy-start.1
  166.4 1.2 copy.9
  167.6 0.4 copy-done.1
  167.9 1.8 bitcast_subtract_fusion
  (11 shorter events, 0.2 us)
Async XLA Ops:
  7.2 93.9 %all-reduce.2.cloned.1.call-start = ((), (), s32[]{:S(2)}) async-start(), calls=%async_computation.2 | async-start | bytes 524288 | tf_op jit(solution)/shard_map/psum | solution.py:22
  10.0 1.3 copy-start
  166.3 1.6 copy-start.1
Sparse Core Ops, SparseCore 0:
  69.7 31.2 all-reduce.1

commit v2 on v0

--- a/solution.py
+++ b/solution.py
@@ -17,7 +17,8 @@
     new_momentum = hold_rate * momentum + gradients
     whole = lax.all_to_all(new_momentum, "rows", split_axis=0, concat_axis=1, tiled=True)
     gram = jnp.einsum("mik,mjk->mij", whole, whole, precision=lax.Precision.HIGHEST)
-    gram = lax.psum(gram, "cols")
+    parts = lax.all_gather(gram, "cols", axis=0, tiled=False)
+    gram = parts.sum(axis=0)
     eye = jnp.eye(gram.shape[-1], dtype=jnp.float32)
     total = jnp.sum(gram * eye, axis=(1, 2), keepdims=True)
     scale = lax.rsqrt(total + 1e-06)

time: 175 us -> 160 us (0.914)
  waiting for transfers between devices: 31.4 us -> 15.8 us
  matrix products: 12.4 us -> 10.3 us
    psum x1 -> x0, waiting for transfers between devices: 31.4 us -> none  [local(): gram = lax.psum(gram, 'cols')]
    all_gather x0 -> x1, waiting for transfers between devices: none -> 15.8 us  [local(): parts = lax.all_gather(gram, 'cols', axis=0, tiled=False)]
    dot_general x15, matrix products: 9.64 us -> 7.57 us  [mul(): return jnp.einsum('mij,mjk->mik', a, b, precision=lax.Precision.HIGHEST)]
where the time goes in v2:
time: 160 us; the launch traced here: 159 us
  blocking collectives  109 us (68%)
  waiting for transfers between devices  15.8 us (10%)
  between operations  14.2 us (9%)
  matrix products  10.3 us (6%)
  other arithmetic  6.56 us (4%)
  local copies, waits for them, and re-layouts  3.17 us (2%)
    all_to_all x1, blocking collectives, local(): lax.all_to_all(new_momentum, 'rows', split_axis=0, concat_axis=1, tiled=T...  55.3 us
    all_to_all x1, blocking collectives, local(): lax.all_to_all(iterate, 'rows', split_axis=1, concat_axis=0, tiled=True)  53.9 us
    all_gather x1, waiting for transfers between devices, local(): parts = lax.all_gather(gram, 'cols', axis=0, tiled=False)  15.8 us
    dot_general x15, matrix products, mul(): return jnp.einsum('mij,mjk->mik', a, b, precision=lax.Precision.HIGHEST)  7.57 us
  transfers between devices with their start and end apart: 1, of which 1 were waited for; matrix products, arithmetic and copies ran while one was open for 0% of the time, Pallas kernels for 0%

profile of v2, /device:TPU:0, one launch (start us, length us, event | category | flops | bytes accessed | tf_op | source)
XLA Modules:
  0.0 159.4 jit_solution(14867783212618348793)
XLA Ops:
  7.2 0.0 all-gather.3.cloned.1.call-start
  7.2 2.7 %multiply_add_fusion = f32[32,16,1024]{2,1,0:T(8,128)S(1)} fusion(f32[32,16,1024]{2,1,0:T(8,128)} %param.3, f32[32,16,1024]{2,1,0:T(8,128)} %param.4), kind=kLoop, calls=%fused_computation.1 | loop fusion | flops 1048576 | bytes 6291456 | tf_op jit(solution)/shard_map/add | solution.py:17
  9.9 0.0 copy-start
  9.9 55.3 %all_to_all.27 = f32[32,16,1024]{2,1,0:T(8,128)S(1)} all-to-all(f32[32,16,1024]{2,1,0:T(8,128)S(1)} %multiply_add_fusion), channel_id=1, replica_groups=mesh['rows'=8,'cols'=4] {'rows'}, dimensions={0} | all-to-all | bytes 4194304 | tf_op jit(solution)/shard_map/all_to_all | solution.py:18
  65.2 0.0 copy-done
  65.2 0.2 copy.7
  65.5 2.8 %fusion.13 = f32[4,128,128]{2,1,0:T(8,128)} fusion(f32[4,128,1024]{2,1,0:T(8,128)S(1)} %bitcast.38), kind=kOutput, calls=%fused_computation.24 | convolution fusion | flops 805306368 | bytes 2359296 | tf_op jit(solution)/shard_map/mik,mjk->mij/dot_general | solution.py:19
  68.2 0.0 all-gather.3.cloned.1.call-update
  68.3 15.8 %all-gather.3.cloned.1.call-done = f32[16,128,128]{2,1,0:T(8,128)} async-done(((f32[4,128,128]{2,1,0:T(8,128)}), f32[16,128,128]{2,1,0:T(8,128)}) %all-gather.3.cloned.1.call-update) | async-done | bytes 1048592 | tf_op jit(solution)/shard_map/all_gather | solution.py:20
  84.1 1.3 reduce_sum.18
  85.4 0.1 multiply_reduce_fusion
  85.6 0.5 fusion.3
  86.1 0.4 fusion.6
  86.5 0.4 fusion.4
  87.0 0.4 fusion.14
  87.4 0.4 fusion.2
  87.7 0.4 fusion.15
  88.1 0.4 fusion.19
  88.5 0.4 fusion.16
  88.9 0.4 fusion.1
  89.3 0.4 fusion.17
  89.7 0.4 fusion.20
  90.1 0.4 fusion.18
  90.5 0.4 fusion
  90.9 0.4 fusion.21
  91.3 1.9 %fusion.22 = f32[4,128,1024]{2,1,0:T(8,128)S(1)} fusion(f32[4,128,128]{2,1,0:T(8,128)S(1)} %fusion.21, f32[4,128,1024]{2,1,0:T(8,128)S(1)} %bitcast.39), kind=kOutput, calls=%fused_computation.33 | convolution fusion | flops 805306368 | bytes 4456448 | tf_op jit(solution)/shard_map/mij,mjk->mik/dot_general | solution.py:13
  93.2 1.4 copy.8
  94.6 53.9 %all_to_all.28 = f32[4,128,1024]{2,0,1:T(4,128)S(1)} all-to-all(f32[4,128,1024]{2,0,1:T(4,128)S(1)} %copy.8), channel_id=1, replica_groups=mesh['rows'=8,'cols'=4] {'rows'}, dimensions={1} | all-to-all | bytes 4194304 | tf_op jit(solution)/shard_map/all_to_all | solution.py:33
  148.5 0.7 broadcast_multiply_fusion
  149.2 0.0 copy-start.1
  149.2 1.2 copy.9
  150.4 0.4 copy-done.1
  150.8 1.8 %bitcast_subtract_fusion = f32[32,16,1024]{2,1,0:T(8,128)} fusion(f32[8,4,16,1024]{3,2,1,0:T(8,128)S(1)} %copy.9, f32[32,16,1024]{2,1,0:T(8,128)S(1)} %copy-done.1), kind=kLoop, calls=%fused_computation | loop fusion | flops 1048576 | bytes 6291456 | tf_op jit(solution)/shard_map/sub | solution.py:34
  (3 shorter events, 0.0 us)
Async XLA Ops:
  7.2 76.9 %all-gather.3.cloned.1.call-start = ((), (), s32[]{:S(2)}) async-start(), calls=%async_computation.2 | async-start | bytes 1310720 | tf_op jit(solution)/shard_map/all_gather | solution.py:20
  9.9 55.4 %copy-start = (f32[32,16,1024]{2,1,0:T(8,128)}, f32[32,16,1024]{2,1,0:T(8,128)S(1)}, u32[]{:S(2)}) copy-start(f32[32,16,1024]{2,1,0:T(8,128)S(1)} %multiply_add_fusion) | copy-start | bytes 6291460
  149.2 1.6 %copy-start.1 = (f32[32,16,1024]{2,1,0:T(8,128)S(1)}, f32[32,16,1024]{2,1,0:T(8,128)}, u32[]{:S(2)}) copy-start(f32[32,16,1024]{2,1,0:T(8,128)} %param.5) | copy-start | bytes 6291460
Sparse Core Ops, SparseCore 0:
  68.4 15.6 all-gather.2
